TPU v7x, 1024 devices: a whole 8x8x8 slice. The times are simulated.
1024 devices in a mesh: dp: 16 (over x_hi, y), mp: 64 (over x_lo, z, core).
Axes of the slice: x: 8 (x_hi: 2, x_lo: 4; x = x_hi * 4 + x_lo), y: 8, z: 8, core: 2. Of those that a mesh axis runs over, the one named last changes fastest.
Arguments:
- inputs: bfloat16 [2048, 6144], P('dp'), may hold values from -6 to 6
- pre_act: bfloat16 [2048, 12288], P('dp', 'mp'), may hold values from -6 to 6
- out_grad: bfloat16 [2048, 6144], P('dp'), may hold values from -6 to 6
- w_in: bfloat16 [6144, 12288], P(None, 'mp'), may hold values from -0.21875 to 0.21875
- w_out: bfloat16 [12288, 6144], P('mp'), may hold values from -0.0546875 to 0.0546875
- master_in: float32 [6144, 12288], P('dp', 'mp'), may hold values from -0.3 to 0.3
- master_out: float32 [12288, 6144], P('mp', 'dp'), may hold values from -0.3 to 0.3
- row_in: float32 [6144], P('dp'), may hold values from 25.6 to 1372.16
- col_in: float32 [12288], P('mp'), may hold values from 51 to 256
- row_out: float32 [12288], P('mp'), may hold values from 51.2 to 2744.32
- col_out: float32 [6144], P('dp'), may hold values from 102 to 512
Outputs:
- input_grad: bfloat16 [2048, 6144], P('dp', 'mp')
- new_master_in: float32 [6144, 12288], P('dp', 'mp')
- new_master_out: float32 [12288, 6144], P('mp', 'dp')
All inputs are finite; a program needn't handle non-finite values.
Results may differ from a plain program's by a relative error of at most 0.012.
Values may be sent and summed in bfloat16 or wider, within the bound.
A program may use at most 64 MiB of HBM per device.

v0:
```python
import math

import jax
import jax.numpy as jnp
from jax import lax
from jax.sharding import Mesh
from jax.sharding import PartitionSpec as P

D = 6144
FF = 12288
DP = ("dp_0", "dp_1")


decay_rate = 0.8
step_size = 0.05
tiny_square = 1e-30


def own_block(blocks, axes, order):
    inside = blocks.shape[1:]
    blocks = blocks.reshape(*(lax.axis_size(a) for a in axes), *inside)
    blocks = jnp.moveaxis(blocks, order, range(len(axes))).reshape(-1, *inside)
    for k in order:
        blocks = lax.psum_scatter(blocks, axes[k], scatter_dimension=0, tiled=True)
    return blocks[0]


def in_blocks(array, dim, devices):
    shape = array.shape
    blocks = array.reshape(*shape[:dim], devices, shape[dim] // devices, *shape[dim + 1 :])
    return jnp.moveaxis(blocks, dim, 0)


def sum_by_axis(array, axes, order, dim):
    devices = lax.axis_size(axes)
    return own_block(in_blocks(array, dim, devices), axes, order)


def from_everyone(array, axis):
    devices = lax.axis_size(axis)
    return lax.all_to_all(
        jnp.broadcast_to(array[None], (devices, *array.shape)), axis, 0, 0, tiled=True
    )


def of_everyone(array, axis):
    everything = from_everyone(array, axis)
    return jnp.sum(everything, axis=0)


def in_one(arrays, axis):
    ends = [0]
    for a in arrays:
        ends.append(ends[-1] + a.size)
    so_far = of_everyone(jnp.concatenate([a.ravel() for a in arrays]), axis)
    return tuple((so_far[b:e].reshape(a.shape) for a, b, e in zip(arrays, ends, ends[1:])))


def gelu_parts(pre):
    cumulative = 0.5 * (1.0 + jax.scipy.special.erf(pre * (1.0 / math.sqrt(2.0))))
    density = jnp.exp(-0.5 * pre * pre) * (1.0 / math.sqrt(2.0 * math.pi))
    return (pre * cumulative, cumulative + pre * density)


def contract_rows(left, right):
    return lax.dot_general(
        left, right, (((0,), (0,)), ((), ())), preferred_element_type=jnp.float32
    )


def body(
    inputs, pre_act, out_grad, w_in, w_out, master_in, master_out, row_in, col_in, row_out, col_out
):
    active, slope = gelu_parts(pre_act.astype(jnp.float32))
    hidden = active.astype(jnp.bfloat16)
    hid_grad = lax.dot_general(
        out_grad, w_out, (((1,), (1,)), ((), ())), preferred_element_type=jnp.float32
    )
    pre_grad = (hid_grad * slope).astype(jnp.bfloat16)
    local_hidden = w_in.shape[1]
    input_cols = lax.psum_scatter(
        lax.dot_general(
            w_in, pre_grad, (((1,), (1,)), ((), ())), preferred_element_type=jnp.float32
        ),
        "mp",
        scatter_dimension=0,
        tiled=True,
    )
    input_grad = input_cols.T.astype(jnp.bfloat16)
    joined = sum_by_axis(
        jnp.concatenate(
            [contract_rows(inputs, pre_grad), contract_rows(out_grad, hidden)], axis=1
        ).astype(jnp.bfloat16),
        DP,
        (1, 0),
        0,
    ).astype(jnp.float32)
    grad_in = joined[:, :local_hidden]
    grad_out = joined[:, local_hidden:].T
    square_in = grad_in * grad_in + tiny_square
    square_out = grad_out * grad_out + tiny_square
    width_in, width_out = in_one((jnp.sum(square_in, axis=1), jnp.sum(square_out, axis=0)), "mp")
    hidden_in, hidden_out = in_one((jnp.sum(square_in, axis=0), jnp.sum(square_out, axis=1)), DP)
    rows_in = decay_rate * row_in + (1.0 - decay_rate) * width_in / FF
    cols_in = decay_rate * col_in + (1.0 - decay_rate) * hidden_in / D
    rows_out = decay_rate * row_out + (1.0 - decay_rate) * hidden_out / D
    cols_out = decay_rate * col_out + (1.0 - decay_rate) * width_out / FF
    mean_in = of_everyone(jnp.sum(rows_in), DP) / D
    mean_out = of_everyone(jnp.sum(rows_out), "mp") / FF
    update_in = grad_in / jnp.sqrt(rows_in[:, None] * cols_in[None, :] / mean_in)
    update_out = grad_out / jnp.sqrt(rows_out[:, None] * cols_out[None, :] / mean_out)
    new_master_in = master_in - step_size * update_in
    new_master_out = master_out - step_size * update_out
    return (input_grad, new_master_in, new_master_out)


def solution(mesh):
    split = Mesh(mesh.devices.reshape(2, 8, mesh.shape["mp"]), ("dp_0", "dp_1", "mp"))
    return jax.shard_map(
        body,
        mesh=split,
        in_specs=(
            P(DP, None),
            P(DP, "mp"),
            P(DP, None),
            P(None, "mp"),
            P("mp", None),
            P(DP, "mp"),
            P("mp", DP),
            P(DP),
            P("mp"),
            P("mp"),
            P(DP),
        ),
        out_specs=(P(DP, "mp"), P(DP, "mp"), P("mp", DP)),
        check_vma=False,
    )
```

profile of v0, /device:TPU:1, one launch (start us, length us, event | category | flops | bytes accessed | tf_op | source)
XLA Modules:
  0.0 456.5 jit_solution(591601091674208411)
XLA Ops:
  7.2 0.0 copy-start
  7.2 0.0 copy-start.5
  7.2 0.0 reduce-scatter.6.cloned.1.call-start
  7.2 0.0 copy-start.1
  7.2 0.0 copy-start.2
  7.3 2.4 convolution_convert_fusion
  9.6 0.0 copy-done.5
  9.6 0.0 copy-done.1
  9.6 0.4 copy-done.2
  10.0 0.8 fusion
  10.8 0.0 copy-start.3
  10.8 0.5 copy.37
  11.3 0.9 copy-done.3
  12.2 0.8 convolution_convert_fusion.1
  13.0 0.5 copy.36
  13.5 0.5 maximum_bitcast_fusion
  14.0 3.2 copy.20
  17.2 0.0 reduce-scatter.6.cloned.1.call-update
  17.2 0.0 reduce-scatter.8.cloned.1.call-start
  17.3 77.6 %reduce-scatter.6.cloned.1.call-done = bf16[2,384,384]{1,2,0:T(8,128)(2,1)} async-done(((bf16[16,384,384]{1,2,0:T(8,128)(2,1)}), bf16[2,384,384]{1,2,0:T(8,128)(2,1)}) %reduce-scatter.6.cloned.1.call-update) | async-done | bytes 589840 | tf_op jit(solution)/shard_map/reduce_scatter | solution.py:24
  94.8 0.0 reduce-scatter.8.cloned.1.call-update
  94.9 0.0 reduce-scatter.10.cloned.1.call-start
  94.9 0.0 copy-done
  94.9 2.3 convolution_bitcast_fusion
  97.2 3.5 copy.26
  100.8 0.0 copy-start.8
  100.8 0.0 copy-start.9
  100.8 0.0 copy-start.6
  100.8 0.0 copy-start.7
  100.8 0.0 copy-start.4
  100.8 0.0 reduce-scatter.10.cloned.1.call-update
  100.8 28.7 %reduce-scatter.8.cloned.1.call-done = bf16[1,384,384]{1,2,0:T(8,128)(2,1)} async-done(((bf16[2,384,384]{1,2,0:T(8,128)(2,1)}), bf16[1,384,384]{1,2,0:T(8,128)(2,1)}) %reduce-scatter.8.cloned.1.call-update) | async-done | bytes 294928 | tf_op jit(solution)/shard_map/reduce_scatter | solution.py:24
  129.5 1.0 bitcast_convert_fusion
  130.5 0.1 fusion.3
  130.7 0.1 fusion.1
  130.8 0.1 pad_maximum_fusion.1
  130.9 17.7 %all_to_all.24 = f32[16,1,384]{2,1,0:T(1,128)S(1)} all-to-all(f32[16,1,384]{2,1,0:T(1,128)S(1)} %broadcast_in_dim.9), channel_id=1, replica_groups=mesh['dp_0'=2,'dp_1'=8,'mp'=64] {'dp_0','dp_1'}, dimensions={0} | all-to-all | bytes 49152 | tf_op jit(solution)/shard_map/all_to_all | solution.py:41
  148.6 0.0 copy-done.8
  148.6 0.0 copy-done.9
  148.6 0.7 fusion.14
  149.3 1.3 broadcast_in_dim.11
  150.6 17.0 %all-to-all-start.3 = ((f32[64,1,1]{2,1,0:T(1,128)}), f32[64,1,1]{2,1,0:T(1,128)S(1)}, u32[]{:S(2)}, u32[]{:S(2)}) async-start(f32[64,1,1]{2,1,0:T(1,128)} %broadcast_in_dim.11), calls=%async_computation.5 | async-start | bytes 65536 | tf_op jit(solution)/shard_map/all_to_all | solution.py:41
  167.6 9.5 %all-to-all-done.3 = f32[64,1,1]{2,1,0:T(1,128)S(1)} async-done(((f32[64,1,1]{2,1,0:T(1,128)}), f32[64,1,1]{2,1,0:T(1,128)S(1)}, u32[]{:S(2)}, u32[]{:S(2)}) %all-to-all-start.3) | async-done | bytes 288 | tf_op jit(solution)/shard_map/all_to_all | solution.py:41
  177.2 0.8 broadcast_in_dim.8
  177.9 4.7 %all-to-all-start = ((f32[64,1,768]{2,1,0:T(1,128)}), f32[64,1,768]{2,1,0:T(1,128)S(1)}, u32[]{:S(2)}, u32[]{:S(2)}) async-start(f32[64,1,768]{2,1,0:T(1,128)} %broadcast_in_dim.8), calls=%async_computation.2 | async-start | bytes 393216 | tf_op jit(solution)/shard_map/all_to_all | solution.py:41
  182.7 239.8 %reduce-scatter.10.cloned.1.call-done = f32[96,128]{1,0:T(8,128)} async-done(((f32[6144,128]{1,0:T(8,128)}), f32[96,128]{1,0:T(8,128)}) %reduce-scatter.10.cloned.1.call-update) | async-done | bytes 49168
  422.4 0.9 copy.27
  423.3 0.7 copy.25
  424.1 0.7 reduce_sum.99
  425.4 0.0 all-to-all-done
  425.4 0.2 reduce_sum.92
  425.5 0.0 copy-done.6
  425.5 0.0 copy-done.7
  425.6 0.6 fusion.15
  426.2 1.2 broadcast_in_dim.10
  427.4 8.3 %all-to-all-start.2 = ((f32[16,1,1]{2,1,0:T(1,128)}), f32[16,1,1]{2,1,0:T(1,128)S(1)}, u32[]{:S(2)}, u32[]{:S(2)}) async-start(f32[16,1,1]{2,1,0:T(1,128)} %broadcast_in_dim.10), calls=%async_computation.4 | async-start | bytes 16384 | tf_op jit(solution)/shard_map/all_to_all | solution.py:41
  435.7 0.0 copy-done.4
  435.7 0.9 multiply_subtract_fusion
  436.6 10.3 %all-to-all-done.2 = f32[16,1,1]{2,1,0:T(1,128)S(1)} async-done(((f32[16,1,1]{2,1,0:T(1,128)}), f32[16,1,1]{2,1,0:T(1,128)S(1)}, u32[]{:S(2)}, u32[]{:S(2)}) %all-to-all-start.2) | async-done | bytes 96 | tf_op jit(solution)/shard_map/all_to_all | solution.py:41
  446.9 0.6 reduce_sum.97
  448.1 1.8 multiply_subtract_fusion.1
  (3 shorter events, 0.1 us)
Async XLA Ops:
  7.2 87.7 %copy-start = (bf16[6144,192]{0,1:T(8,128)(2,1)S(1)}, bf16[6144,192]{0,1:T(8,128)(2,1)}, u32[]{:S(2)}) copy-start(bf16[6144,192]{0,1:T(8,128)(2,1)} %param.14) | copy-start | bytes 7077892
  7.2 2.4 copy-start.5
  7.2 87.6 %reduce-scatter.6.cloned.1.call-start = ((), (), s32[]{:S(2)}) async-start(), calls=%async_computation.7 | async-start | bytes 5308416 | tf_op jit(solution)/shard_map/reduce_scatter | solution.py:24
  7.2 2.4 copy-start.1
  7.2 2.7 copy-start.2
  10.8 1.4 copy-start.3
  17.2 112.3 %reduce-scatter.8.cloned.1.call-start = ((), (), s32[]{:S(2)}) async-start(), calls=%async_computation.8 | async-start | bytes 884736 | tf_op jit(solution)/shard_map/reduce_scatter | solution.py:24
  94.9 327.6 %reduce-scatter.10.cloned.1.call-start = ((), (), s32[]{:S(2)}) async-start(), calls=%async_computation.9 | async-start | bytes 3194880
  100.8 47.9 %copy-start.8 = (f32[192]{0:T(256)S(1)}, f32[192]{0:T(256)}, u32[]{:S(2)}) copy-start(f32[192]{0:T(256)} %param.20) | copy-start | bytes 2308
  100.8 47.9 %copy-start.9 = (f32[192]{0:T(256)S(1)}, f32[192]{0:T(256)}, u32[]{:S(2)}) copy-start(f32[192]{0:T(256)} %param.19) | copy-start | bytes 2308
  100.8 324.8 %copy-start.6 = (f32[384]{0:T(512)S(1)}, f32[384]{0:T(512)}, u32[]{:S(2)}) copy-start(f32[384]{0:T(512)} %param.18) | copy-start | bytes 4612
  100.8 324.8 %copy-start.7 = (f32[384]{0:T(512)S(1)}, f32[384]{0:T(512)}, u32[]{:S(2)}) copy-start(f32[384]{0:T(512)} %param.21) | copy-start | bytes 4612
  100.8 334.9 %copy-start.4 = (f32[192,384]{1,0:T(8,128)S(1)}, f32[192,384]{1,0:T(8,128)}, u32[]{:S(2)}) copy-start(f32[192,384]{1,0:T(8,128)} %param.17) | copy-start | bytes 884740
  150.6 26.6 %all-to-all-start.3 = ((f32[64,1,1]{2,1,0:T(1,128)}), f32[64,1,1]{2,1,0:T(1,128)S(1)}, u32[]{:S(2)}, u32[]{:S(2)}) async-start(f32[64,1,1]{2,1,0:T(1,128)} %broadcast_in_dim.11), calls=%async_computation.5 | async-start | bytes 65536 | tf_op jit(solution)/shard_map/all_to_all | solution.py:41
  177.9 247.4 %all-to-all-start = ((f32[64,1,768]{2,1,0:T(1,128)}), f32[64,1,768]{2,1,0:T(1,128)S(1)}, u32[]{:S(2)}, u32[]{:S(2)}) async-start(f32[64,1,768]{2,1,0:T(1,128)} %broadcast_in_dim.8), calls=%async_computation.2 | async-start | bytes 393216 | tf_op jit(solution)/shard_map/all_to_all | solution.py:41
  427.4 19.4 %all-to-all-start.2 = ((f32[16,1,1]{2,1,0:T(1,128)}), f32[16,1,1]{2,1,0:T(1,128)S(1)}, u32[]{:S(2)}, u32[]{:S(2)}) async-start(f32[16,1,1]{2,1,0:T(1,128)} %broadcast_in_dim.10), calls=%async_computation.4 | async-start | bytes 16384 | tf_op jit(solution)/shard_map/all_to_all | solution.py:41
Sparse Core Ops, SparseCore 0:
  17.3 77.4 reduce-scatter.5
  98.2 31.2 reduce-scatter.7
  132.9 289.4 reduce-scatter.9
where the time goes:
time: 461 us; the launch traced here: 456 us
  waiting for transfers between devices  366 us (79%)
  starting transfers between devices  30.1 us (7%)
  blocking collectives  17.7 us (4%)
  between operations  15.3 us (3%)
  local copies, waits for them, and re-layouts  14 us (3%)
  other arithmetic  7.29 us (2%)
  matrix products  6.18 us (1%)
    unnamed x4, waiting for transfers between devices  240 us
    reduce_scatter x2, waiting for transfers between devices, own_block(): blocks = lax.psum_scatter(blocks, axes[k], scatter_dimension=0, tiled=True)  106 us
    all_to_all x3, starting transfers between devices, from_everyone(): lax.all_to_all(jnp.broadcast_to(array[None], (devices, *array.shape)), ax...  30 us
    all_to_all x3, waiting for transfers between devices, from_everyone(): lax.all_to_all(jnp.broadcast_to(array[None], (devices, *array.shape)), ax...  19.9 us
    all_to_all x1, blocking collectives, from_everyone(): lax.all_to_all(jnp.broadcast_to(array[None], (devices, *array.shape)), ax...  17.7 us
  transfers between devices with their start and end apart: 6, of which 5 were waited for; matrix products, arithmetic and copies ran while one was open for 3% of the time, Pallas kernels for 0%

commit v1 on v0

v1 whole, which is shorter than its diff:
```python
import math

import jax
import jax.numpy as jnp
from jax import lax
from jax.experimental import pallas as pl
from jax.experimental.pallas import tpu as pltpu
from jax.sharding import PartitionSpec as P

MESH = pl.DeviceIdType.MESH
BF = jnp.bfloat16
F32 = jnp.float32
D = 6144
FF = 12288
TOK = 128
COLS = 384
HID = 192
OUTC = 96
RT = 16
DECAY = 0.8
STEP = 0.05
TINY = 1e-30


def xor2(a, k):
    return ((a // 2 + k // 2) % 2) * 2 + (a % 2 + k % 2) % 2


def slot(other, dy):
    dy = dy % 8
    chunk = (3 if dy % 2 else 0) if other else (2 if dy % 2 else 1)
    return (chunk * 4 + dy // 2) * TOK


def schedule(direction):
    last = (0, 1) if direction == 0 else (2, 3)
    return [(hop, k) for hop in (1, 2, 3) for k in range(4)] + [(4, k) for k in last]


def following(direction, n):
    if n < 8:
        return n + 4
    if n < 12:
        k = n - 8
        if direction == 0 and k < 2:
            return 12 + k
        if direction == 1 and k >= 2:
            return 12 + k - 2
    return None


KINDS = ((1, 0), (0, 0), (1, 1), (0, 1))


def kernel(
    x_hbm, pre_hbm, g_hbm, win_hbm, wout_hbm, min_hbm, mout_hbm, rin_hbm, cin_hbm, rout_hbm, cout_hbm,
    ig_out, nmi_out, nmo_out,
    pre_v, g_v, win_v, wout_v, min_v, mout_v, rin_v, cin_v, rout_v, cout_v,
    xg, hp, p_v, qown, a0s, a0r, a1s, a1r, a2s, a2r, fold, stw, sth, wr0, wr1, hr1, wr2, hr2, tr3,
    lsem, s1s, s1r, s2s, s2r, zs, zr, ys, yr, cs, cr, xs, xr,
    a0ss, a0rs, a1ss, a1rs, a2ss, a2rs, t0s, t0r, t1s, t1r, u1s, u1r, t2s, t2r, u2s, u2r, t3s, t3r,
):
    dp = lax.axis_index("dp")
    mp = lax.axis_index("mp")
    h, y = dp // 8, dp % 8
    a, z, c = mp // 16, (mp // 2) % 8, mp % 2
    x = h * 4 + a

    def at(xx, yy, zz, cc):
        xx, yy, zz = xx % 8, yy % 8, zz % 8
        return ((xx // 4) * 8 + yy, (xx % 4) * 16 + zz * 2 + cc)

    def remote(src, dst, ss, rs, dev):
        return pltpu.make_async_remote_copy(
            src_ref=src, dst_ref=dst, send_sem=ss, recv_sem=rs, device_id=dev, device_id_type=MESH
        )

    partner = at(x, y, z, 1 - c)
    loads = [
        pltpu.make_async_copy(s, d, lsem.at[i])
        for i, (s, d) in enumerate(
            (
                (pre_hbm, pre_v), (g_hbm, g_v), (wout_hbm, wout_v), (win_hbm, win_v), (min_hbm, min_v),
                (mout_hbm, mout_v), (rin_hbm, rin_v), (cin_hbm, cin_v), (rout_hbm, rout_v), (cout_hbm, cout_v),
            )
        )
    ]
    for cp in loads:
        cp.start()

    a_far = 3 - a
    x_far = (1 - h) * 4 + a_far
    greet = [at(x + k, y, z, c) for k in range(1, 8)]
    greet += [at(x, y + k, z, c) for k in range(1, 8)]
    greet += [at(x, y, z + k, c) for k in range(1, 8)]
    greet += [at(x, y, z + k, 1 - c) for k in range(8)]
    greet += [at(x_far, y + k, z, c) for k in range(1, 8)]
    barrier = pltpu.get_barrier_semaphore()
    for dev in greet:
        pl.semaphore_signal(barrier, inc=1, device_id=dev, device_id_type=MESH)

    loads[0].wait()
    pre = pre_v[...].astype(F32)
    cumulative = 0.5 * (1.0 + lax.erf(pre * (1.0 / math.sqrt(2.0))))
    density = jnp.exp(-0.5 * pre * pre) * (1.0 / math.sqrt(2.0 * math.pi))
    own = slot(0, 0)
    hp[1, :, own : own + TOK] = (pre * cumulative).astype(BF)
    slope = cumulative + pre * density

    pl.semaphore_wait(barrier, len(greet))

    near = (a + 1) // 2 % 2 == 1
    q_to = jnp.where(near, a, a_far)
    x_to = jnp.where(near, x, x_far)
    odd = q_to // 2

    def s1_copy(src, idx):
        y_to = (y - (2 * idx + odd)) % 8
        j = (x_to // 4) * 8 + y_to
        piece = src.at[pl.ds(pl.multiple_of(RT * z, RT), RT), pl.ds(pl.multiple_of(COLS * j, COLS), COLS)]
        return piece, xg.at[c, q_to, idx, z], at(x_to, y_to, z, c)

    def s1_start(src):
        for idx in range(4):
            piece, there, dev = s1_copy(src, idx)

            def far_copy():
                remote(piece, there, s1s.at[idx], s1r.at[idx], dev).start()

            if idx == 0:

                @pl.when(a == 1)
                def _():
                    pltpu.make_async_copy(piece, there, s1r.at[idx]).start()

                pl.when(a != 1)(far_copy)
            else:
                far_copy()

    @pl.when(c == 0)
    def _():
        s1_start(x_hbm)

    @pl.when(c == 1)
    def _():
        s1_start(g_hbm)

    def y_msg(d, n):
        hop, kind = schedule(d)[n]
        of, other = KINDS[kind]
        sgn = 1 if d == 0 else -1
        b, e = slot(other, -sgn * (hop - 1)), slot(other, -sgn * hop)
        return remote(
            hp.at[of, :, b : b + TOK], hp.at[of, :, e : e + TOK], ys.at[d, n], yr.at[d, n], at(x, y + sgn, z, c)
        )

    def cross(of):
        b, e = slot(0, 0), slot(1, 0)
        return remote(hp.at[of, :, b : b + TOK], hp.at[of, :, e : e + TOK], xs.at[of], xr.at[of], at(x + 4, y, z, c))

    cross(1).start()
    for d in (0, 1):
        y_msg(d, 0).start()

    loads[1].wait()
    loads[2].wait()
    hid_grad = lax.dot_general(wout_v[...], g_v[...], (((1,), (1,)), ((), ())), preferred_element_type=F32)
    pre_grad = hid_grad * slope
    hp[0, :, own : own + TOK] = pre_grad.astype(BF)
    p_v[...] = jnp.transpose(pre_grad).astype(BF)
    cross(0).start()
    for d in (0, 1):
        y_msg(d, 1).start()

    def piece_of(k, zo):
        return xg.at[c, xor2(a, k), :, zo % 8]

    def z_msg(d, n):
        hop, k = schedule(d)[n]
        sgn = 1 if d == 0 else -1
        ref = piece_of(k, z - sgn * (hop - 1))
        return remote(ref, ref, zs.at[d, n], zr.at[d, n], at(x, y, z + sgn, c))

    def share(k, rel):
        ref = piece_of(k, z + rel)
        return remote(ref, ref, cs.at[k, rel % 8], cr.at[k, rel % 8], partner)

    for idx in range(4):
        pltpu.make_async_copy(xg.at[c, a, idx, z], xg.at[c, a, idx, z], s1r.at[idx]).wait()

    def s2_msg(k):
        ref = piece_of(0, z)
        return remote(ref, ref, s2s.at[k - 1], s2r.at[k - 1], at(h * 4 + xor2(a, k), y, z, c))

    for k in (1, 2, 3):
        s2_msg(k).start()
    for k in range(4):
        if k:
            s2_msg(k).wait_recv()
        for d in (0, 1):
            z_msg(d, k).start()
        share(k, 0).start()

    cross(1).wait_recv()
    for d in (0, 1):
        y_msg(d, 2).start()

    loads[3].wait()

    def product(k, half):
        at_col = pl.multiple_of(1536 * xor2(a, k) + 768 * half, 128)
        return jnp.dot(p_v[...], win_v[:, pl.ds(at_col, 768)], preferred_element_type=F32)

    def a0_msg(k):
        return remote(a0s.at[k], a0r.at[k], a0ss.at[k], a0rs.at[k], partner)

    for k in (1, 2, 3, 0):
        a0s[k] = product(k, 1 - c).astype(BF)
        a0_msg(k).start()

    cross(0).wait_recv()
    for d in (0, 1):
        y_msg(d, 3).start()

    def tick(n):
        for d in (0, 1):
            hop, k = schedule(d)[n]
            sgn = 1 if d == 0 else -1
            after = following(d, n)
            z_msg(d, n).wait_recv()
            if after is not None:
                z_msg(d, after).start()
            share(k, -sgn * hop).start()
        for d in (0, 1):
            after = following(d, n)
            y_msg(d, n).wait_recv()
            if after is not None:
                y_msg(d, after).start()

    def a1_msg(k):
        return remote(
            a1s.at[k - 1], a1r.at[k - 1], a1ss.at[k - 1], a1rs.at[k - 1], at(h * 4 + xor2(a, k), y, z, c)
        )

    tick(0)
    for k in (1, 2, 3, 0):
        mine = product(k, c)
        a0_msg(k).wait_recv()
        mine = mine + a0r[k].astype(F32)
        if k:
            a1s[k - 1] = mine.astype(BF)
            a1_msg(k).start()
        else:
            qown[...] = mine
        tick({1: 1, 2: 2, 3: 3, 0: 4}[k])
    for n in range(5, 14):
        tick(n)
    for k in range(4):
        for rel in range(8):
            share(k, rel).wait_recv()

    def gradient(of):
        total = jnp.zeros((HID, COLS), F32)
        for q in range(4):
            total += jnp.dot(
                hp[of, :, 512 * q : 512 * (q + 1)], xg[of, q].reshape(512, COLS), preferred_element_type=F32
            )
        return total

    grad_in = gradient(0)
    grad_out = gradient(1)

    def thirds(v):
        return v[:, :128], v[:, 128:256], v[:, 256:]

    for cp in loads[4:]:
        cp.wait()
    fold[...] = jnp.zeros_like(fold)
    stw[0] = jnp.zeros((8, 128), F32)
    sth[0] = jnp.zeros((8, 128), F32)
    rout_row = rout_v[...]
    lasts = []
    for s, grad in enumerate((grad_in, grad_out)):
        square = grad * grad + TINY
        wide = jnp.sum(square, axis=0, keepdims=True)
        for i, part in enumerate(thirds(wide)):
            stw[0, 3 * s + i : 3 * s + i + 1, :] = part
        w0, w1, w2 = thirds(wide)
        lasts.append(((1.0 - DECAY) / (D * FF)) * (w0 + w1 + w2))
        s0, s1, s2 = thirds(square)
        fold[s, 0:HID, :] = s0 + s1 + s2
        row = jnp.sum(jnp.transpose(fold[s]), axis=0, keepdims=True)
        sth[0, 2 * s : 2 * s + 1, :] = row[:, :128]
        sth[0, 2 * s + 1 : 2 * s + 2, :] = row[:, 128:]
    r0, r1, r2 = thirds(rin_v[...])
    stw[0, 6:7, :] = lasts[0] + (DECAY / (64 * D)) * (r0 + r1 + r2)
    lane = lax.broadcasted_iota(jnp.int32, (1, 128), 1)
    tail = jnp.concatenate([rout_row[:, 128:], rout_row[:, 128:]], axis=1)
    tail = jnp.where(lane < 64, tail, 0.0)
    stw[0, 7:8, :] = lasts[1] + (DECAY / (16 * FF)) * (rout_row[:, :128] + tail)

    m0 = remote(stw.at[0], wr0, t0s, t0r, partner)
    m0.start()
    h1 = [remote(sth.at[0], hr1.at[k - 1], u1s.at[k - 1], u1r.at[k - 1], at(x, y + k, z, c)) for k in range(1, 8)]
    for m in h1:
        m.start()
    m0.wait_recv()
    w1 = stw[0] + wr0[...]
    stw[1] = w1
    z1 = [remote(stw.at[1], wr1.at[k - 1], t1s.at[k - 1], t1r.at[k - 1], at(x, y, z + k, c)) for k in range(1, 8)]
    for m in z1:
        m.start()

    part = qown[...]
    for k in (1, 2, 3):
        a1_msg(k).wait_recv()
        part = part + a1r[k - 1].astype(F32)
    a2s[...] = jnp.transpose(part).astype(BF).reshape(8, OUTC, TOK)

    h_sum = sth[0]
    for k, m in enumerate(h1):
        m.wait_recv()
        h_sum = h_sum + hr1[k]
    sth[1] = h_sum
    h2 = remote(sth.at[1], hr2, u2s, u2r, at(x + 4, y, z, c))
    h2.start()
    for k, m in enumerate(z1):
        m.wait_recv()
        w1 = w1 + wr1[k]
    stw[2] = w1
    x2 = [remote(stw.at[2], wr2.at[k - 1], t2s.at[k - 1], t2r.at[k - 1], at(x + k, y, z, c)) for k in range(1, 8)]
    for m in x2:
        m.start()

    def a2_dest(b):
        return 4 * c + b // 2, b % 2

    for b in range(8):
        zz, cc = a2_dest(b)
        mine = jnp.logical_and(zz == z, cc == c)

        @pl.when(mine)
        def _():
            pltpu.make_async_copy(a2s.at[b], a2r.at[z], a2rs.at[z]).start()

        @pl.when(jnp.logical_not(mine))
        def _():
            remote(a2s.at[b], a2r.at[z], a2ss.at[b], a2rs.at[z], at(x, y, zz, cc)).start()

    w_mp = w1
    w_all = w1
    for k, m in enumerate(x2, start=1):
        m.wait_recv()
        got = wr2[k - 1]
        same = ((x - k + 8) % 8) // 4 == h
        w_mp = w_mp + jnp.where(same, got, 0.0)
        w_all = w_all + got
    stw[3] = w_all
    y3 = [remote(stw.at[3], tr3.at[k - 1], t3s.at[k - 1], t3r.at[k - 1], at(x, y + k, z, c)) for k in range(1, 8)]
    for m in y3:
        m.start()
    h2.wait_recv()
    h_sum = h_sum + hr2[...]

    def lanes(t, first):
        return jnp.concatenate([t[first + i : first + i + 1, :] for i in range(3)], axis=1)

    def column(row):
        fold[0, 0:128, :] = jnp.broadcast_to(row[:, :128], (128, 128))
        fold[1, 0:128, :] = jnp.broadcast_to(row[:, 128:], (128, 128))
        return jnp.concatenate([jnp.transpose(fold[0, 0:128, :]), jnp.transpose(fold[1, 0:128, :])[:64]], axis=0)

    def hidden_row(t, first):
        return jnp.concatenate([t[first : first + 1, :], t[first + 1 : first + 2, :]], axis=1)

    def padded(v):
        end = jnp.concatenate([v[:, 128:], v[:, 128:]], axis=1)
        return jnp.concatenate([v[:, :128], end], axis=1)

    rows_in = DECAY * rin_v[...] + ((1.0 - DECAY) / FF) * lanes(w_mp, 0)
    cols_out = DECAY * cout_v[...] + ((1.0 - DECAY) / FF) * lanes(w_mp, 3)
    cols_in = DECAY * padded(cin_v[...]) + ((1.0 - DECAY) / D) * hidden_row(h_sum, 0)
    rows_out = DECAY * padded(rout_v[...]) + ((1.0 - DECAY) / D) * hidden_row(h_sum, 2)
    col_in = column(lax.rsqrt(cols_in))
    col_out = column(lax.rsqrt(rows_out))
    scaled_in = grad_in * lax.rsqrt(rows_in) * jnp.concatenate([col_in] * 3, axis=1)
    scaled_out = grad_out * lax.rsqrt(cols_out) * jnp.concatenate([col_out] * 3, axis=1)

    for k in range(8):
        pltpu.make_async_copy(a2r.at[k], a2r.at[k], a2rs.at[k]).wait()
    total = a2r[0].astype(F32)
    for k in range(1, 8):
        total = total + a2r[k].astype(F32)
    ig_out[...] = total.astype(BF)

    for k, m in enumerate(y3):
        m.wait_recv()
        w_all = w_all + tr3[k]
    mean_in = jnp.sum(w_all[6:7, :], axis=1, keepdims=True)
    mean_out = jnp.sum(w_all[7:8, :], axis=1, keepdims=True)
    nmi_out[...] = min_v[...] - scaled_in * (STEP * jnp.sqrt(mean_in))
    nmo_out[...] = mout_v[...] - scaled_out * (STEP * jnp.sqrt(mean_out))

    @pl.when(a != 1)
    def _():
        remote(xg.at[c, a, 0, z], xg.at[c, a, 0, z], s1s.at[0], s1r.at[0], partner).wait_send()

    for idx in range(1, 4):
        remote(xg.at[c, a, idx, z], xg.at[c, a, idx, z], s1s.at[idx], s1r.at[idx], partner).wait_send()
    for k in (1, 2, 3):
        s2_msg(k).wait_send()
        a1_msg(k).wait_send()
    for k in range(4):
        a0_msg(k).wait_send()
        for rel in range(8):
            share(k, rel).wait_send()
    for d in (0, 1):
        for n in range(14):
            z_msg(d, n).wait_send()
            y_msg(d, n).wait_send()
    cross(0).wait_send()
    cross(1).wait_send()
    for m in (m0, h2, *h1, *z1, *x2, *y3):
        m.wait_send()
    for b in range(8):
        zz, cc = a2_dest(b)

        @pl.when(jnp.logical_not(jnp.logical_and(zz == z, cc == c)))
        def _():
            remote(a2s.at[b], a2r.at[b], a2ss.at[b], a2rs.at[b], partner).wait_send()


def body(
    inputs, pre_act, out_grad, w_in, w_out, master_in, master_out, row_in, col_in, row_out, col_out
):
    dma = pltpu.SemaphoreType.DMA
    vm = pltpu.VMEM
    out = pl.pallas_call(
        kernel,
        name="backward_step",
        out_shape=(
            jax.ShapeDtypeStruct((OUTC, TOK), BF),
            jax.ShapeDtypeStruct((HID, COLS), F32),
            jax.ShapeDtypeStruct((HID, COLS), F32),
        ),
        in_specs=[pl.BlockSpec(memory_space=pl.ANY)] * 11,
        out_specs=[pl.BlockSpec(memory_space=pltpu.VMEM)] * 3,
        scratch_shapes=[
            vm((HID, TOK), BF), vm((TOK, D), BF), vm((HID, D), BF), vm((HID, D), BF),
            vm((HID, COLS), F32), vm((HID, COLS), F32),
            vm((1, COLS), F32), vm((1, HID), F32), vm((1, HID), F32), vm((1, COLS), F32),
            vm((2, 4, 4, 8, RT, COLS), BF), vm((2, HID, 2048), BF), vm((TOK, HID), BF),
            vm((TOK, 768), F32), vm((4, TOK, 768), BF), vm((4, TOK, 768), BF),
            vm((3, TOK, 768), BF), vm((3, TOK, 768), BF), vm((8, OUTC, TOK), BF), vm((8, OUTC, TOK), BF),
            vm((2, 256, 128), F32), vm((4, 8, 128), F32), vm((2, 8, 128), F32),
            vm((8, 128), F32), vm((7, 8, 128), F32), vm((7, 8, 128), F32), vm((7, 8, 128), F32),
            vm((8, 128), F32), vm((7, 8, 128), F32),
            dma((10,)), dma((4,)), dma((4,)), dma((3,)), dma((3,)),
            dma((2, 14)), dma((2, 14)), dma((2, 14)), dma((2, 14)), dma((4, 8)), dma((4, 8)), dma((2,)), dma((2,)),
            dma((4,)), dma((4,)), dma((3,)), dma((3,)), dma((8,)), dma((8,)),
            dma, dma, dma((7,)), dma((7,)), dma((7,)), dma((7,)), dma((7,)), dma((7,)), dma, dma,
            dma((7,)), dma((7,)),
        ],
        compiler_params=pltpu.CompilerParams(
            collective_id=0, has_side_effects=True, vmem_limit_bytes=48 * 2**20
        ),
    )(
        inputs, pre_act.T, out_grad, w_in.T, w_out, master_in.T, master_out,
        row_in.reshape(1, COLS), col_in.reshape(1, HID), row_out.reshape(1, HID), col_out.reshape(1, COLS),
    )
    return out[0].T, out[1].T, out[2]


def solution(mesh):
    return jax.shard_map(
        body,
        mesh=mesh,
        in_specs=(
            P("dp", None),
            P("dp", "mp"),
            P("dp", None),
            P(None, "mp"),
            P("mp", None),
            P("dp", "mp"),
            P("mp", "dp"),
            P("dp"),
            P("mp"),
            P("mp"),
            P("dp"),
        ),
        out_specs=(P("dp", "mp"), P("dp", "mp"), P("mp", "dp")),
        check_vma=False,
    )
```

time: 461 us -> 84.7 us (0.18)
  waiting for transfers between devices: 366 us -> 0 us
  Pallas kernels: 0 us -> 73.4 us
  starting transfers between devices: 30.1 us -> 0 us
  blocking collectives: 17.7 us -> 0 us
  between operations: 15.3 us -> 0.65 us
  other arithmetic: 7.29 us -> 0 us
  matrix products: 6.18 us -> 0 us
    unnamed x4 -> x0, waiting for transfers between devices: 240 us -> none
    reduce_scatter x2 -> x0, waiting for transfers between devices: 106 us -> none  [own_block(): blocks = lax.psum_scatter(blocks, axes[k], scatter_dimension=0, tiled=True)]
    pallas_call x0 -> x1, Pallas kernels: none -> 73.4 us  [body(): pl.pallas_call(kernel, name='backward_step', out_shape=(jax.ShapeDtypeStr...]
    all_to_all x3 -> x0, starting transfers between devices: 30 us -> none  [from_everyone(): lax.all_to_all(jnp.broadcast_to(array[None], (devices, *array.shape)), ax...]
    all_to_all x3 -> x0, waiting for transfers between devices: 19.9 us -> none  [from_everyone(): lax.all_to_all(jnp.broadcast_to(array[None], (devices, *array.shape)), ax...]
    all_to_all x1 -> x0, blocking collectives: 17.7 us -> none  [from_everyone(): lax.all_to_all(jnp.broadcast_to(array[None], (devices, *array.shape)), ax...]
    dot_general x4 -> x0, matrix products: 6.18 us -> none  [the longest x2 3.12 us: contract_rows(): lax.dot_general(left, right, (((0,), (0,)), ((), ())), preferred_element_...]
  transfers between devices with their start and end apart: 6 -> 0, of which waited for: 5 -> 0; matrix products, arithmetic and copies ran while one was open for 3% -> 0% of each run, Pallas kernels for 0% -> 0%
where the time goes in v1:
time: 84.7 us; the launch traced here: 84.3 us
  Pallas kernels  73.4 us (87%)
  local copies, waits for them, and re-layouts  10.3 us (12%)
    pallas_call x1, Pallas kernels, body(): pl.pallas_call(kernel, name='backward_step', out_shape=(jax.ShapeDtypeStr...  73.4 us
    unnamed x17, local copies, waits for them, and re-layouts  8.93 us

profile of v1, /device:TPU:1, one launch (start us, length us, event | category | flops | bytes accessed | tf_op | source)
XLA Modules:
  0.0 84.3 jit_solution(7695215359317107898)
XLA Ops:
  0.6 0.7 reshape.18.rin_hbm
  1.3 0.7 reshape.21.cout_hbm
  2.0 0.0 copy-start
  2.0 1.4 %copy-done = bf16[128,6144]{1,0:T(8,128)(2,1)S(1)} copy-done((bf16[128,6144]{1,0:T(8,128)(2,1)S(1)}, bf16[128,6144]{1,0:T(8,128)(2,1)}, u32[]{:S(2)}) %copy-start) | copy-done | bytes 1572888
  3.4 0.0 copy-start.1
  3.4 1.4 %copy-done.1 = bf16[128,6144]{1,0:T(8,128)(2,1)S(1)} copy-done((bf16[128,6144]{1,0:T(8,128)(2,1)S(1)}, bf16[128,6144]{1,0:T(8,128)(2,1)}, u32[]{:S(2)}) %copy-start.1) | copy-done | bytes 1572888
  4.8 0.0 copy-start.2
  4.8 1.0 %copy-done.2 = f32[384,192]{0,1:T(8,128)S(1)} copy-done((f32[384,192]{0,1:T(8,128)S(1)}, f32[384,192]{0,1:T(8,128)}, u32[]{:S(2)}) %copy-start.2) | copy-done | bytes 294936
  5.8 0.0 copy-start.3
  5.8 1.0 %copy-done.3 = f32[192,384]{1,0:T(8,128)S(1)} copy-done((f32[192,384]{1,0:T(8,128)S(1)}, f32[192,384]{1,0:T(8,128)}, u32[]{:S(2)}) %copy-start.3) | copy-done | bytes 294936
  6.7 0.0 copy-start.4
  6.7 0.8 copy-done.4
  7.5 0.0 copy-start.5
  7.5 0.7 copy-done.5
  8.2 0.0 copy-start.6
  8.2 0.7 copy-done.6
  8.9 73.4 %backward_step.1 = (bf16[96,128]{1,0:T(8,128)(2,1)S(1)}, f32[192,384]{1,0:T(8,128)S(1)}, f32[192,384]{1,0:T(8,128)S(1)}) custom-call(bf16[128,6144]{1,0:T(8,128)(2,1)S(1)} %copy-done, bf16[192,128]{1,0:T(8,128)(2,1)S(1)} %bitcast.9, bf16[128,6144]{1,0:T(8,128)(2,1)S(1)} %copy-done.1, bf16[192,6144]{1,0:T(8,128)(2,1)} %bitcast.13, ...), custom_call_target="tpu_custom_call" | custom-call | tf_op jit(solution)/shard_map/backward_step/pallas_call | solution.py:438
  82.3 0.6 copy.17
  82.9 0.7 copy.18
  83.6 0.7 copy.19
Async XLA Ops:
  2.0 1.4 %copy-start = (bf16[128,6144]{1,0:T(8,128)(2,1)S(1)}, bf16[128,6144]{1,0:T(8,128)(2,1)}, u32[]{:S(2)}) copy-start(bf16[128,6144]{1,0:T(8,128)(2,1)} %x_hbm.1) | copy-start | bytes 4718596
  3.4 1.4 %copy-start.1 = (bf16[128,6144]{1,0:T(8,128)(2,1)S(1)}, bf16[128,6144]{1,0:T(8,128)(2,1)}, u32[]{:S(2)}) copy-start(bf16[128,6144]{1,0:T(8,128)(2,1)} %g_hbm.1) | copy-start | bytes 4718596
  4.8 1.0 %copy-start.2 = (f32[384,192]{0,1:T(8,128)S(1)}, f32[384,192]{0,1:T(8,128)}, u32[]{:S(2)}) copy-start(f32[384,192]{0,1:T(8,128)} %param.16) | copy-start | bytes 884740
  5.8 1.0 %copy-start.3 = (f32[192,384]{1,0:T(8,128)S(1)}, f32[192,384]{1,0:T(8,128)}, u32[]{:S(2)}) copy-start(f32[192,384]{1,0:T(8,128)} %mout_hbm.1) | copy-start | bytes 884740
  6.7 0.8 copy-start.4
  7.5 0.7 copy-start.5
  8.2 0.7 copy-start.6

commit v2 on v0

v2 whole, which is shorter than its diff:
```python
import math

import jax
import jax.numpy as jnp
from jax import lax
from jax.experimental import pallas as pl
from jax.experimental.pallas import tpu as pltpu
from jax.sharding import PartitionSpec as P

MESH = pl.DeviceIdType.MESH
BF = jnp.bfloat16
F32 = jnp.float32
D = 6144
FF = 12288
TOK = 128
COLS = 384
HID = 192
OUTC = 96
RT = 16
PARTS = 4
KP = D // PARTS
DECAY = 0.8
STEP = 0.05
TINY = 1e-30

NEAR = (0, 1, 7, 2)
FAR = (6, 3, 5, 4)
KINDS = ((1, 0), (0, 0), (1, 1), (0, 1))
LAST = ((0, 3), (1, 2))
ORDER = (
    [("a0", 1), ("a0", 2), ("a0", 3), ("a0", 0), ("s1", 0), ("y", 1, 0), ("s1", 1), ("cross", 1), ("y", 1, 1)]
    + [("s2", 2), ("z", 1, 0), ("a1", 1), ("y", 2, 0), ("s2", 3), ("z", 1, 1), ("a1", 2), ("cross", 0)]
    + [("y", 1, 2), ("z", 1, 2), ("a1", 3), ("y", 2, 1), ("z", 2, 0), ("a1", 0), ("y", 3, 0), ("z", 1, 3)]
    + [("y", 1, 3), ("z", 2, 1), ("y", 2, 2), ("z", 2, 2), ("y", 3, 1), ("z", 3, 0), ("y", 4, 0), ("y", 2, 3)]
    + [("z", 2, 3), ("y", 3, 2), ("z", 3, 1), ("z", 3, 2), ("y", 4, 1), ("y", 3, 3), ("z", 4, 0), ("z", 3, 3)]
    + [("y", 4, 2), ("z", 4, 1), ("z", 4, 2), ("y", 4, 3), ("z", 4, 3)]
)


def xor2(a, k):
    return ((a // 2 + k // 2) % 2) * 2 + (a % 2 + k % 2) % 2


def slot(other, dy):
    dy = dy % 8
    half, place = (0, NEAR.index(dy)) if dy in NEAR else (1, FAR.index(dy))
    return ((other * 2 + half) * 4 + place) * TOK


def message(hop, k):
    return (hop - 1) * 4 + k


def kernel(
    x_hbm, pre_hbm, g_hbm, win_hbm, wout_hbm, min_hbm, mout_hbm, rin_hbm, cin_hbm, rout_hbm, cout_hbm,
    ig_out, nmi_out, nmo_out,
    pre_v, g_v, win_v, wout_v, min_v, mout_v, rin_v, cin_v, rout_v, cout_v,
    xg, hp, p_v, qown, a0s, a0r, a1s, a1r, a2s, a2r, fin, fold, stw, sth, sc_r, sx_r, sz_r, sy_r, st_r, sv_r, hy_r, hx_r,
    lsem, psem, s1s, s1r, s2s, s2r, zs, zr, ys, yr, cs, cr, xs, xr,
    a0ss, a0rs, a1ss, a1rs, a2ss, a2rs, fs, fr, sts, str_, bsem,
):
    dp = lax.axis_index("dp")
    mp = lax.axis_index("mp")
    h, y = dp // 8, dp % 8
    a, z, c = mp // 16, (mp // 2) % 8, mp % 2
    x = h * 4 + a
    inner = (a + 1) // 2 % 2
    is_inner = inner == 1
    is_outer = inner == 0

    def at(xx, yy, zz, cc):
        xx, yy, zz = xx % 8, yy % 8, zz % 8
        return ((xx // 4) * 8 + yy, (xx % 4) * 16 + zz * 2 + cc)

    def remote(src, dst, ss, rs, dev):
        return pltpu.make_async_remote_copy(
            src_ref=src, dst_ref=dst, send_sem=ss, recv_sem=rs, device_id=dev, device_id_type=MESH
        )

    def arrived(ref, sem):
        pltpu.make_async_copy(ref, ref, sem).wait()

    partner = at(x, y, z, 1 - c)
    pair = at(h * 4 + xor2(a, 1), y, z, c)
    x_far = (1 - h) * 4 + 3 - a
    first = [pltpu.make_async_copy(pre_hbm, pre_v, lsem.at[0])]
    parts = []
    for i in range(PARTS):
        cut = slice(i * KP, (i + 1) * KP)
        parts.append(pltpu.make_async_copy(g_hbm.at[:, cut], g_v.at[:, cut], psem.at[i]))
        parts.append(pltpu.make_async_copy(wout_hbm.at[:, cut], wout_v.at[:, cut], psem.at[i]))
    for cp in first + parts:
        cp.start()

    barrier = pltpu.get_barrier_semaphore()

    def greet(dev):
        pl.semaphore_signal(barrier, inc=1, device_id=dev, device_id_type=MESH)

    for k in (4, 3, 5, 2, 6, 1, 7):
        greet(at(x + k, y, z, c))
        greet(at(x, y + k, z, c))
        greet(at(x, y, z + k, c))
    greet(partner)

    @pl.when(is_outer)
    def _():
        for k in (4, 3, 5, 2, 6, 1, 7):
            greet(at(x_far, y + k, z, c))

    loads = [
        pltpu.make_async_copy(s, d, lsem.at[i + 1])
        for i, (s, d) in enumerate(
            (
                (win_hbm, win_v), (min_hbm, min_v), (mout_hbm, mout_v),
                (rin_hbm, rin_v), (cin_hbm, cin_v), (rout_hbm, rout_v), (cout_hbm, cout_v),
            )
        )
    ]
    for cp in loads:
        cp.start()

    first[0].wait()
    pre = pre_v[...].astype(F32)
    cumulative = 0.5 * (1.0 + lax.erf(pre * (1.0 / math.sqrt(2.0))))
    density = jnp.exp(-0.5 * pre * pre) * (1.0 / math.sqrt(2.0 * math.pi))
    own = slot(0, 0)
    hp[1, :, own : own + TOK] = (pre * cumulative).astype(BF)
    slope = cumulative + pre * density

    pl.semaphore_wait(barrier, 22 + 7 * (1 - inner))

    def y_msg(d, hop, kind):
        of, other = KINDS[kind]
        sgn = 1 if d == 0 else -1
        n = message(hop, kind) if hop < 4 else 12 + LAST[d].index(kind)
        b, e = slot(other, -sgn * (hop - 1)), slot(other, -sgn * hop)
        return remote(hp.at[of, :, b : b + TOK], hp.at[of, :, e : e + TOK], ys, yr.at[d, n], at(x, y + sgn, z, c))

    def cross(of):
        b, e = slot(0, 0), slot(1, 0)
        return remote(hp.at[of, :, b : b + TOK], hp.at[of, :, e : e + TOK], xs, xr.at[of], at(x + 4, y, z, c))

    cross(1).start()

    set_q = 2 * (1 - inner)

    def s1_start(src):
        def piece(dy):
            y_to = (y - dy) % 8
            half, place = (0, NEAR.index(dy)) if dy in NEAR else (1, FAR.index(dy))
            x_to = jnp.where(is_inner, x, x_far)
            j = (x_to // 4) * 8 + y_to
            there = xg.at[c, set_q + half, place, z]
            cut = src.at[pl.ds(pl.multiple_of(RT * z, RT), RT), pl.ds(pl.multiple_of(COLS * j, COLS), COLS)]
            return cut, there, s1r.at[half], at(x_to, y_to, z, c)

        def one(dy):
            cut, there, sem, dev = piece(dy)
            remote(cut, there, s1s, sem, dev).start()

        @pl.when(is_inner)
        def _():
            cut, there, sem, _ = piece(0)
            pltpu.make_async_copy(cut, there, sem).start()

        @pl.when(is_outer)
        def _():
            one(0)

        for dy in (1, 7, 2, 6, 3, 5, 4):
            one(dy)

    @pl.when(c == 0)
    def _():
        s1_start(x_hbm)

    @pl.when(c == 1)
    def _():
        s1_start(g_hbm)

    for d in (0, 1):
        y_msg(d, 1, 0).start()

    hid_grad = jnp.zeros((HID, TOK), F32)
    for i in range(PARTS):
        cut = slice(i * KP, (i + 1) * KP)
        parts[2 * i].wait()
        parts[2 * i + 1].wait()
        hid_grad += lax.dot_general(wout_v[:, cut], g_v[:, cut], (((1,), (1,)), ((), ())), preferred_element_type=F32)
    pre_grad = hid_grad * slope
    hp[0, :, own : own + TOK] = pre_grad.astype(BF)
    p_v[...] = jnp.transpose(pre_grad).astype(BF)
    cross(0).start()
    for d in (0, 1):
        y_msg(d, 1, 1).start()

    def chunk(k):
        return (set_q + k) % 4

    def piece_of(k, zo):
        return xg.at[c, chunk(k), :, zo % 8]

    def z_msg(d, hop, k):
        sgn = 1 if d == 0 else -1
        n = message(hop, k) if hop < 4 else 12 + LAST[d].index(k)
        ref = piece_of(k, z - sgn * (hop - 1))
        return remote(ref, ref, zs, zr.at[d, n], at(x, y, z + sgn, c))

    def share(k, rel):
        ref = piece_of(k, z + rel)
        return remote(ref, ref, cs, cr.at[k], partner)

    def s2_msg(k):
        ref = piece_of(k, z)
        return remote(ref, ref, s2s, s2r.at[k], pair)

    def product(k, half):
        at_col = pl.multiple_of(1536 * xor2(a, k) + 768 * half, 128)
        return jnp.dot(p_v[...], win_v[:, pl.ds(at_col, 768)], preferred_element_type=F32)

    def a0_msg(k):
        return remote(a0s.at[k], a0r.at[k], a0ss, a0rs.at[k], partner)

    def a1_msg(k):
        return remote(a1s.at[k - 1], a1r.at[k - 1], a1ss, a1rs, at(h * 4 + xor2(a, k), y, z, c))

    loads[0].wait()
    for event in ORDER:
        what, *rest = event
        if what == "s1":
            (k,) = rest
            arrived(piece_of(k, z), s1r.at[k])
            s2_msg(k).start()
            for d in (0, 1):
                z_msg(d, 1, k).start()
            share(k, 0).start()
        elif what == "s2":
            (k,) = rest
            s2_msg(k - 2).wait_recv()
            for d in (0, 1):
                z_msg(d, 1, k).start()
            share(k, 0).start()
        elif what == "cross":
            (of,) = rest
            cross(of).wait_recv()
            for d in (0, 1):
                y_msg(d, 1, 2 if of == 1 else 3).start()
        elif what in ("y", "z"):
            hop, k = rest
            make = y_msg if what == "y" else z_msg
            for d in (0, 1):
                sgn = 1 if d == 0 else -1
                if hop == 4 and k not in LAST[d]:
                    continue
                make(d, hop, k).wait_recv()
                if hop < 3 or (hop == 3 and k in LAST[d]):
                    make(d, hop + 1, k).start()
                if what == "z":
                    share(k, -sgn * hop).start()
        elif what == "a0":
            (k,) = rest
            a0s[k] = product(k, 1 - c).astype(BF)
            a0_msg(k).start()
        elif what == "a1":
            (k,) = rest
            mine = product(k, c)
            a0_msg(k).wait_recv()
            mine = mine + a0r[k].astype(F32)
            if k:
                a1s[k - 1] = mine.astype(BF)
                a1_msg(k).start()
            else:
                qown[...] = mine
    for k in range(4):
        arrived(xg.at[1 - c, chunk(k)], cr.at[k])

    def gradient(of):
        total = jnp.zeros((HID, COLS), F32)
        for q in range(4):
            total += jnp.dot(
                hp[of, :, 512 * q : 512 * (q + 1)], xg[of, q].reshape(512, COLS), preferred_element_type=F32
            )
        return total

    grad_in = gradient(0)
    grad_out = gradient(1)

    def thirds(v):
        return v[:, :128], v[:, 128:256], v[:, 256:]

    for cp in loads[1:]:
        cp.wait()
    fold[...] = jnp.zeros_like(fold)
    sth[0] = jnp.zeros((8, 128), F32)
    rout_row = rout_v[...]
    lasts = []
    for s, grad in enumerate((grad_in, grad_out)):
        square = grad * grad + TINY
        wide = jnp.sum(square, axis=0, keepdims=True)
        w0, w1, w2 = thirds(wide)
        for i, part in enumerate((w0, w1, w2)):
            stw[0, 3 * s + i : 3 * s + i + 1, :] = part
        lasts.append(((1.0 - DECAY) / (D * FF)) * (w0 + w1 + w2))
        s0, s1, s2 = thirds(square)
        fold[s, 0:HID, :] = s0 + s1 + s2
        row = jnp.sum(jnp.transpose(fold[s]), axis=0, keepdims=True)
        sth[0, 2 * s : 2 * s + 1, :] = row[:, :128]
        sth[0, 2 * s + 1 : 2 * s + 2, :] = row[:, 128:]
    r0, r1, r2 = thirds(rin_v[...].reshape(1, COLS))
    stw[0, 6:7, :] = lasts[0] + (DECAY / (64 * D)) * (r0 + r1 + r2)
    lane = lax.broadcasted_iota(jnp.int32, (1, 128), 1)
    tail = jnp.concatenate([rout_row[:, 128:], rout_row[:, 128:]], axis=1)
    tail = jnp.where(lane < 64, tail, 0.0)
    stw[0, 7:8, :] = lasts[1] + (DECAY / (16 * FF)) * (rout_row[:, :128] + tail)

    def ring_of(axis, k):
        return at(x + k * (axis == "x"), y + k * (axis == "y"), z + k * (axis == "z"), c)

    def spread(src, dst, i, axis):
        ms = [remote(src, dst.at[k - 1], sts, str_.at[i], ring_of(axis, k)) for k in (4, 3, 5, 2, 6, 1, 7)]
        for m in ms:
            m.start()

    m0 = remote(stw.at[0], sc_r, sts, str_.at[0], partner)
    m0.start()
    spread(sth.at[0], hy_r, 1, "y")
    m0.wait_recv()
    w_sum = stw[0] + sc_r[...]
    stw[1] = w_sum
    spread(stw.at[1], sx_r, 2, "x")

    arrived(a1r, a1rs)
    part = qown[...]
    for k in range(3):
        part = part + a1r[k].astype(F32)
    a2s[...] = jnp.transpose(part).astype(BF).reshape(4, 2 * OUTC, TOK)

    arrived(hy_r, str_.at[1])
    h_sum = sth[0]
    for k in range(7):
        h_sum = h_sum + hy_r[k]
    sth[1] = h_sum
    hx = remote(sth.at[1], hx_r, sts, str_.at[3], at(x + 4, y, z, c))
    hx.start()

    arrived(sx_r, str_.at[2])
    w_mp = w_sum
    t_sum = w_sum
    for k in range(1, 8):
        got = sx_r[k - 1]
        same = ((x - k + 8) % 8) // 4 == h
        w_mp = w_mp + jnp.where(same, got, 0.0)
        t_sum = t_sum + got
    stw[2] = t_sum
    spread(stw.at[2, pl.ds(6, 2)], sy_r, 4, "y")
    stw[3] = w_mp
    spread(stw.at[3], sz_r, 5, "z")

    for b in range(4):
        zz = 4 * c + b

        @pl.when(zz == z)
        def _():
            pltpu.make_async_copy(a2s.at[b], a2r.at[z], a2rs).start()

        @pl.when(zz != z)
        def _():
            remote(a2s.at[b], a2r.at[z], a2ss, a2rs, at(x, y, zz, c)).start()

    arrived(sy_r, str_.at[4])
    t_two = t_sum[6:8, :]
    for k in range(7):
        t_two = t_two + sy_r[k]
    st_r[7] = t_two
    spread(st_r.at[7], sv_r, 6, "z")

    arrived(sz_r, str_.at[5])
    for k in range(7):
        w_mp = w_mp + sz_r[k]
    hx.wait_recv()
    h_sum = h_sum + hx_r[...]

    def lanes(t, first_row):
        return jnp.concatenate([t[first_row + i : first_row + i + 1, :] for i in range(3)], axis=1)

    def column(row):
        fold[0, 0:128, :] = jnp.broadcast_to(row[:, :128], (128, 128))
        fold[1, 0:128, :] = jnp.broadcast_to(row[:, 128:], (128, 128))
        return jnp.concatenate([jnp.transpose(fold[0, 0:128, :]), jnp.transpose(fold[1, 0:128, :])[:64]], axis=0)

    def hidden_row(t, first_row):
        return jnp.concatenate([t[first_row : first_row + 1, :], t[first_row + 1 : first_row + 2, :]], axis=1)

    def padded(v):
        end = jnp.concatenate([v[:, 128:], v[:, 128:]], axis=1)
        return jnp.concatenate([v[:, :128], end], axis=1)

    rows_in = DECAY * rin_v[...].reshape(1, COLS) + ((1.0 - DECAY) / FF) * lanes(w_mp, 0)
    cols_out = DECAY * cout_v[...].reshape(1, COLS) + ((1.0 - DECAY) / FF) * lanes(w_mp, 3)
    cols_in = DECAY * padded(cin_v[...]) + ((1.0 - DECAY) / D) * hidden_row(h_sum, 0)
    rows_out = DECAY * padded(rout_v[...]) + ((1.0 - DECAY) / D) * hidden_row(h_sum, 2)
    col_in = column(lax.rsqrt(cols_in))
    col_out = column(lax.rsqrt(rows_out))
    scaled_in = grad_in * lax.rsqrt(rows_in) * jnp.concatenate([col_in] * 3, axis=1)
    scaled_out = grad_out * lax.rsqrt(cols_out) * jnp.concatenate([col_out] * 3, axis=1)

    collects = z // 4 == c

    def last_msg():
        return remote(fin, ig_out, fs, fr, partner)

    @pl.when(collects)
    def _():
        arrived(a2r, a2rs)
        total = a2r[0].astype(F32)
        for k in range(1, 8):
            total = total + a2r[k].astype(F32)
        upper, lower = total[:OUTC].astype(BF), total[OUTC:].astype(BF)

        @pl.when(c == 0)
        def _():
            ig_out[...] = upper
            fin[...] = lower

        @pl.when(c == 1)
        def _():
            ig_out[...] = lower
            fin[...] = upper

        last_msg().start()
        last_msg().wait_send()

    @pl.when(jnp.logical_not(collects))
    def _():
        last_msg().wait_recv()

    @pl.when(is_inner)
    def _():
        arrived(xg.at[c, 0, 0, 0:7], s1s)

    @pl.when(is_outer)
    def _():
        arrived(xg.at[c, 0, 0], s1s)

    arrived(xg.at[c, 0:2, :, 0], s2s)
    arrived(a0s, a0ss)
    arrived(a1s, a1ss)
    arrived(xg.at[c], cs)
    arrived(xg.at[c, :, :, 0:7], zs)
    arrived(hp.at[:, :, 0:1792], ys)
    arrived(hp.at[:, :, 0:TOK], xs)

    @pl.when(collects)
    def _():
        arrived(a2s.at[0:3], a2ss)

    @pl.when(jnp.logical_not(collects))
    def _():
        arrived(a2s, a2ss)

    arrived(sv_r, str_.at[6])
    for k in range(7):
        t_two = t_two + sv_r[k]
    mean_in = jnp.sum(t_two[0:1, :], axis=1, keepdims=True)
    mean_out = jnp.sum(t_two[1:2, :], axis=1, keepdims=True)
    nmi_out[...] = min_v[...] - scaled_in * (STEP * jnp.sqrt(mean_in))
    nmo_out[...] = mout_v[...] - scaled_out * (STEP * jnp.sqrt(mean_out))
    for ref in (stw.at[0], hy_r, sx_r, hx_r, sz_r):
        arrived(ref, sts)
    arrived(sy_r, sts)
    arrived(sv_r, sts)


def put_out(ig, nmi, nmo, ig_out, nmi_out, nmo_out, sem):
    copies = [
        pltpu.make_async_copy(s, d, sem.at[i]) for i, (s, d) in enumerate(((nmi, nmi_out), (nmo, nmo_out), (ig, ig_out)))
    ]
    for cp in copies:
        cp.start()
    for cp in copies:
        cp.wait()


def body(
    inputs, pre_act, out_grad, w_in, w_out, master_in, master_out, row_in, col_in, row_out, col_out
):
    dma = pltpu.SemaphoreType.DMA
    vm = pltpu.VMEM
    shapes = (
        jax.ShapeDtypeStruct((OUTC, TOK), BF),
        jax.ShapeDtypeStruct((HID, COLS), F32),
        jax.ShapeDtypeStruct((HID, COLS), F32),
    )
    made = pl.pallas_call(
        kernel,
        name="backward_step",
        out_shape=shapes,
        in_specs=[pl.BlockSpec(memory_space=pl.ANY)] * 11,
        out_specs=[pl.BlockSpec(memory_space=pltpu.VMEM)] * 3,
        scratch_shapes=[
            vm((HID, TOK), BF), vm((TOK, D), BF), vm((HID, D), BF), vm((HID, D), BF),
            vm((HID, COLS), F32), vm((HID, COLS), F32),
            vm((COLS,), F32), vm((1, HID), F32), vm((1, HID), F32), vm((COLS,), F32),
            vm((2, 4, 4, 8, RT, COLS), BF), vm((2, HID, 2048), BF), vm((TOK, HID), BF),
            vm((TOK, 768), F32), vm((4, TOK, 768), BF), vm((4, TOK, 768), BF),
            vm((3, TOK, 768), BF), vm((3, TOK, 768), BF), vm((4, 2 * OUTC, TOK), BF), vm((8, 2 * OUTC, TOK), BF),
            vm((OUTC, TOK), BF),
            vm((2, 256, 128), F32), vm((4, 8, 128), F32), vm((2, 8, 128), F32),
            vm((8, 128), F32), vm((7, 8, 128), F32), vm((7, 8, 128), F32), vm((7, 2, 128), F32),
            vm((8, 2, 128), F32), vm((7, 2, 128), F32), vm((7, 8, 128), F32), vm((8, 128), F32),
            dma((8,)), dma((PARTS,)), dma, dma((2,)), dma, dma((2,)),
            dma, dma((2, 14)), dma, dma((2, 14)), dma, dma((4,)), dma, dma((2,)),
            dma, dma((4,)), dma, dma, dma, dma, dma, dma, dma, dma((7,)), dma,
        ],
        compiler_params=pltpu.CompilerParams(
            collective_id=0, has_side_effects=True, vmem_limit_bytes=48 * 2**20
        ),
    )(
        *(
            pltpu.with_memory_space_constraint(v, pltpu.HBM)
            for v in (
                inputs, pre_act.T, out_grad, w_in.T, w_out, master_in.T, master_out,
                row_in, col_in.reshape(1, HID), row_out.reshape(1, HID), col_out,
            )
        )
    )
    out = pl.pallas_call(
        put_out,
        name="put_out",
        out_shape=shapes,
        in_specs=[pl.BlockSpec(memory_space=pl.ANY)] * 3,
        out_specs=[pl.BlockSpec(memory_space=pl.ANY)] * 3,
        scratch_shapes=[dma((3,))],
        compiler_params=pltpu.CompilerParams(vmem_limit_bytes=2**20),
    )(*made)
    return out[0].T, out[1].T, out[2]


def solution(mesh):
    return jax.shard_map(
        body,
        mesh=mesh,
        in_specs=(
            P("dp", None),
            P("dp", "mp"),
            P("dp", None),
            P(None, "mp"),
            P("mp", None),
            P("dp", "mp"),
            P("mp", "dp"),
            P("dp"),
            P("mp"),
            P("mp"),
            P("dp"),
        ),
        out_specs=(P("dp", "mp"), P("dp", "mp"), P("mp", "dp")),
        check_vma=False,
    )
```

time: 461 us -> 71.5 us (0.16)
  waiting for transfers between devices: 366 us -> 0 us
  Pallas kernels: 0 us -> 70.4 us
  starting transfers between devices: 30.1 us -> 0 us
  blocking collectives: 17.7 us -> 0 us
  between operations: 15.3 us -> 0.64 us
  local copies, waits for them, and re-layouts: 14 us -> 0 us
  other arithmetic: 7.29 us -> 0 us
  matrix products: 6.18 us -> 0 us
    unnamed x4 -> x0, waiting for transfers between devices: 240 us -> none
    reduce_scatter x2 -> x0, waiting for transfers between devices: 106 us -> none  [own_block(): blocks = lax.psum_scatter(blocks, axes[k], scatter_dimension=0, tiled=True)]
    pallas_call x0 -> x2, Pallas kernels: none -> 70.4 us  [the longest x1 69.5 us: body(): pl.pallas_call(kernel, name='backward_step', out_shape=shapes, in_specs=[...]
    all_to_all x3 -> x0, starting transfers between devices: 30 us -> none  [from_everyone(): lax.all_to_all(jnp.broadcast_to(array[None], (devices, *array.shape)), ax...]
    all_to_all x3 -> x0, waiting for transfers between devices: 19.9 us -> none  [from_everyone(): lax.all_to_all(jnp.broadcast_to(array[None], (devices, *array.shape)), ax...]
    all_to_all x1 -> x0, blocking collectives: 17.7 us -> none  [from_everyone(): lax.all_to_all(jnp.broadcast_to(array[None], (devices, *array.shape)), ax...]
    unnamed x25 -> x0, local copies, waits for them, and re-layouts: 7.45 us -> none
    dot_general x4 -> x0, matrix products: 6.18 us -> none  [the longest x2 3.12 us: contract_rows(): lax.dot_general(left, right, (((0,), (0,)), ((), ())), preferred_element_...]
  transfers between devices with their start and end apart: 6 -> 0, of which waited for: 5 -> 0; matrix products, arithmetic and copies ran while one was open for 3% -> 0% of each run, Pallas kernels for 0% -> 0%
where the time goes in v2:
time: 71.5 us; the launch traced here: 71 us
  Pallas kernels  70.4 us (98%)
    pallas_call x1, Pallas kernels, body(): pl.pallas_call(kernel, name='backward_step', out_shape=shapes, in_specs=[...  69.5 us

profile of v2, /device:TPU:1, one launch (start us, length us, event | category | flops | bytes accessed | tf_op | source)
XLA Modules:
  0.0 71.0 jit_solution(7270301620639285626)
XLA Ops:
  0.6 69.5 %backward_step.1 = (bf16[96,128]{1,0:T(8,128)(2,1)S(1)}, f32[192,384]{1,0:T(8,128)S(1)}, f32[192,384]{1,0:T(8,128)S(1)}) custom-call(bf16[128,6144]{1,0:T(8,128)(2,1)} %x_hbm.1, bf16[192,128]{1,0:T(8,128)(2,1)} %bitcast.9, bf16[128,6144]{1,0:T(8,128)(2,1)} %g_hbm.1, bf16[192,6144]{1,0:T(8,128)(2,1)} %bitcast.7, bf16[192,6144]{1,0:T(8,128)(2,1)} %wout_hbm.1, ...), custom_call_target="tpu_custom_call" | custom-call | tf_op jit(solution)/shard_map/backward_step/pallas_call | solution.py:495
  70.2 0.8 %put_out.1 = (bf16[96,128]{1,0:T(8,128)(2,1)}, f32[192,384]{1,0:T(8,128)}, f32[192,384]{1,0:T(8,128)}) custom-call(bf16[96,128]{1,0:T(8,128)(2,1)S(1)} %get-tuple-element.9.ig, f32[192,384]{1,0:T(8,128)S(1)} %get-tuple-element.10.nmi, f32[192,384]{1,0:T(8,128)S(1)} %get-tuple-element.11.nmo), custom_call_target="tpu_custom_call" | custom-call | tf_op jit(solution)/shard_map/put_out/pallas_call | solution.py:528

commit v3 on v2

--- a/solution.py
+++ b/solution.py
@@ -28,12 +28,12 @@
 KINDS = ((1, 0), (0, 0), (1, 1), (0, 1))
 LAST = ((0, 3), (1, 2))
 ORDER = (
-    [("a0", 1), ("a0", 2), ("a0", 3), ("a0", 0), ("s1", 0), ("y", 1, 0), ("s1", 1), ("cross", 1), ("y", 1, 1)]
-    + [("s2", 2), ("z", 1, 0), ("a1", 1), ("y", 2, 0), ("s2", 3), ("z", 1, 1), ("a1", 2), ("cross", 0)]
-    + [("y", 1, 2), ("z", 1, 2), ("a1", 3), ("y", 2, 1), ("z", 2, 0), ("a1", 0), ("y", 3, 0), ("z", 1, 3)]
-    + [("y", 1, 3), ("z", 2, 1), ("y", 2, 2), ("z", 2, 2), ("y", 3, 1), ("z", 3, 0), ("y", 4, 0), ("y", 2, 3)]
-    + [("z", 2, 3), ("y", 3, 2), ("z", 3, 1), ("z", 3, 2), ("y", 4, 1), ("y", 3, 3), ("z", 4, 0), ("z", 3, 3)]
-    + [("y", 4, 2), ("z", 4, 1), ("z", 4, 2), ("y", 4, 3), ("z", 4, 3)]
+    [("a0", 1), ("a0", 2), ("a0", 3), ("a0", 0), ("y", 1, 0), ("s1", 0), ("cross", 1), ("y", 1, 1), ("s1", 1)]
+    + [("cross", 0), ("y", 2, 0), ("a1", 1), ("s2", 2), ("y", 1, 2), ("z", 1, 0), ("a1", 2), ("y", 2, 1), ("s2", 3)]
+    + [("z", 1, 1), ("y", 1, 3), ("a1", 3), ("y", 3, 0), ("z", 1, 2), ("y", 2, 2), ("a1", 0), ("z", 2, 0)]
+    + [("z", 1, 3), ("y", 3, 1), ("z", 2, 1), ("y", 2, 3), ("z", 2, 2), ("y", 4, 0), ("y", 3, 2), ("z", 3, 0)]
+    + [("z", 2, 3), ("y", 4, 1), ("y", 3, 3), ("z", 3, 1), ("z", 3, 2), ("y", 4, 2), ("z", 4, 0), ("z", 3, 3)]
+    + [("y", 4, 3), ("z", 4, 1), ("z", 4, 2), ("z", 4, 3)]
 )
 
 
@@ -55,7 +55,7 @@
     x_hbm, pre_hbm, g_hbm, win_hbm, wout_hbm, min_hbm, mout_hbm, rin_hbm, cin_hbm, rout_hbm, cout_hbm,
     ig_out, nmi_out, nmo_out,
     pre_v, g_v, win_v, wout_v, min_v, mout_v, rin_v, cin_v, rout_v, cout_v,
-    xg, hp, p_v, qown, a0s, a0r, a1s, a1r, a2s, a2r, fin, fold, stw, sth, sc_r, sx_r, sz_r, sy_r, st_r, sv_r, hy_r, hx_r,
+    xg, hp, p_v, qown, a0s, a0r, a1s, a1r, a2s, a2r, fin, src_v, fold, stw, sth, sc_r, sx_r, sz_r, sy_r, st_r, sv_r, hy_r, hx_r,
     lsem, psem, s1s, s1r, s2s, s2r, zs, zr, ys, yr, cs, cr, xs, xr,
     a0ss, a0rs, a1ss, a1rs, a2ss, a2rs, fs, fr, sts, str_, bsem,
 ):
@@ -89,6 +89,16 @@
         cut = slice(i * KP, (i + 1) * KP)
         parts.append(pltpu.make_async_copy(g_hbm.at[:, cut], g_v.at[:, cut], psem.at[i]))
         parts.append(pltpu.make_async_copy(wout_hbm.at[:, cut], wout_v.at[:, cut], psem.at[i]))
+    rows = pl.ds(pl.multiple_of(RT * z, RT), RT)
+
+    @pl.when(c == 0)
+    def _():
+        pltpu.make_async_copy(x_hbm.at[rows], src_v, bsem).start()
+
+    @pl.when(c == 1)
+    def _():
+        pltpu.make_async_copy(g_hbm.at[rows], src_v, bsem).start()
+
     for cp in first + parts:
         cp.start()
 
@@ -100,7 +110,8 @@
     for k in (4, 3, 5, 2, 6, 1, 7):
         greet(at(x + k, y, z, c))
         greet(at(x, y + k, z, c))
-        greet(at(x, y, z + k, c))
+    greet(at(x, y, z + 1, c))
+    greet(at(x, y, z + 7, c))
     greet(partner)
 
     @pl.when(is_outer)
@@ -128,7 +139,7 @@
     hp[1, :, own : own + TOK] = (pre * cumulative).astype(BF)
     slope = cumulative + pre * density
 
-    pl.semaphore_wait(barrier, 22 + 7 * (1 - inner))
+    pl.semaphore_wait(barrier, 17 + 7 * (1 - inner))
 
     def y_msg(d, hop, kind):
         of, other = KINDS[kind]
@@ -145,39 +156,31 @@
 
     set_q = 2 * (1 - inner)
 
-    def s1_start(src):
-        def piece(dy):
-            y_to = (y - dy) % 8
-            half, place = (0, NEAR.index(dy)) if dy in NEAR else (1, FAR.index(dy))
-            x_to = jnp.where(is_inner, x, x_far)
-            j = (x_to // 4) * 8 + y_to
-            there = xg.at[c, set_q + half, place, z]
-            cut = src.at[pl.ds(pl.multiple_of(RT * z, RT), RT), pl.ds(pl.multiple_of(COLS * j, COLS), COLS)]
-            return cut, there, s1r.at[half], at(x_to, y_to, z, c)
-
-        def one(dy):
-            cut, there, sem, dev = piece(dy)
-            remote(cut, there, s1s, sem, dev).start()
-
-        @pl.when(is_inner)
-        def _():
-            cut, there, sem, _ = piece(0)
-            pltpu.make_async_copy(cut, there, sem).start()
-
-        @pl.when(is_outer)
-        def _():
-            one(0)
-
-        for dy in (1, 7, 2, 6, 3, 5, 4):
-            one(dy)
-
-    @pl.when(c == 0)
-    def _():
-        s1_start(x_hbm)
-
-    @pl.when(c == 1)
-    def _():
-        s1_start(g_hbm)
+    def piece(dy):
+        y_to = (y - dy) % 8
+        half, place = (0, NEAR.index(dy)) if dy in NEAR else (1, FAR.index(dy))
+        x_to = jnp.where(is_inner, x, x_far)
+        j = (x_to // 4) * 8 + y_to
+        there = xg.at[c, set_q + half, place, z]
+        return src_v.at[:, pl.ds(pl.multiple_of(COLS * j, COLS), COLS)], there, s1r.at[half], at(x_to, y_to, z, c)
+
+    def one(dy):
+        cut, there, sem, dev = piece(dy)
+        remote(cut, there, s1s, sem, dev).start()
+
+    arrived(src_v, bsem)
+
+    @pl.when(is_inner)
+    def _():
+        cut, there, sem, _ = piece(0)
+        pltpu.make_async_copy(cut, there, sem).start()
+
+    @pl.when(is_outer)
+    def _():
+        one(0)
+
+    for dy in (1, 7, 2, 6, 3, 5, 4):
+        one(dy)
 
     for d in (0, 1):
         y_msg(d, 1, 0).start()
@@ -335,6 +338,16 @@
     for k in range(3):
         part = part + a1r[k].astype(F32)
     a2s[...] = jnp.transpose(part).astype(BF).reshape(4, 2 * OUTC, TOK)
+    for b in range(4):
+        zz = 4 * c + b
+
+        @pl.when(zz == z)
+        def _():
+            pltpu.make_async_copy(a2s.at[b], a2r.at[z], a2rs).start()
+
+        @pl.when(zz != z)
+        def _():
+            remote(a2s.at[b], a2r.at[z], a2ss, a2rs, at(x, y, zz, c)).start()
 
     arrived(hy_r, str_.at[1])
     h_sum = sth[0]
@@ -356,17 +369,6 @@
     spread(stw.at[2, pl.ds(6, 2)], sy_r, 4, "y")
     stw[3] = w_mp
     spread(stw.at[3], sz_r, 5, "z")
-
-    for b in range(4):
-        zz = 4 * c + b
-
-        @pl.when(zz == z)
-        def _():
-            pltpu.make_async_copy(a2s.at[b], a2r.at[z], a2rs).start()
-
-        @pl.when(zz != z)
-        def _():
-            remote(a2s.at[b], a2r.at[z], a2ss, a2rs, at(x, y, zz, c)).start()
 
     arrived(sy_r, str_.at[4])
     t_two = t_sum[6:8, :]
@@ -505,7 +507,7 @@
             vm((2, 4, 4, 8, RT, COLS), BF), vm((2, HID, 2048), BF), vm((TOK, HID), BF),
             vm((TOK, 768), F32), vm((4, TOK, 768), BF), vm((4, TOK, 768), BF),
             vm((3, TOK, 768), BF), vm((3, TOK, 768), BF), vm((4, 2 * OUTC, TOK), BF), vm((8, 2 * OUTC, TOK), BF),
-            vm((OUTC, TOK), BF),
+            vm((OUTC, TOK), BF), vm((RT, D), BF),
             vm((2, 256, 128), F32), vm((4, 8, 128), F32), vm((2, 8, 128), F32),
             vm((8, 128), F32), vm((7, 8, 128), F32), vm((7, 8, 128), F32), vm((7, 2, 128), F32),
             vm((8, 2, 128), F32), vm((7, 2, 128), F32), vm((7, 8, 128), F32), vm((8, 128), F32),

time: 71.5 us -> 69.8 us (0.976)
  Pallas kernels: 70.4 us -> 68 us
    pallas_call x1, Pallas kernels: 69.5 us -> 67.1 us  [body(): pl.pallas_call(kernel, name='backward_step', out_shape=shapes, in_specs=[...]
where the time goes in v3:
time: 69.8 us; the launch traced here: 68.6 us
  Pallas kernels  68 us (97%)
    pallas_call x1, Pallas kernels, body(): pl.pallas_call(kernel, name='backward_step', out_shape=shapes, in_specs=[...  67.1 us

profile of v3, /device:TPU:1, one launch (start us, length us, event | category | flops | bytes accessed | tf_op | source)
XLA Modules:
  0.0 68.6 jit_solution(3089905476898721630)
XLA Ops:
  0.6 67.1 %backward_step.1 = (bf16[96,128]{1,0:T(8,128)(2,1)S(1)}, f32[192,384]{1,0:T(8,128)S(1)}, f32[192,384]{1,0:T(8,128)S(1)}) custom-call(bf16[128,6144]{1,0:T(8,128)(2,1)} %x_hbm.1, bf16[192,128]{1,0:T(8,128)(2,1)} %bitcast.9, bf16[128,6144]{1,0:T(8,128)(2,1)} %g_hbm.1, bf16[192,6144]{1,0:T(8,128)(2,1)} %bitcast.7, bf16[192,6144]{1,0:T(8,128)(2,1)} %wout_hbm.1, ...), custom_call_target="tpu_custom_call" | custom-call | tf_op jit(solution)/shard_map/backward_step/pallas_call | solution.py:497
  67.8 0.8 %put_out.1 = (bf16[96,128]{1,0:T(8,128)(2,1)}, f32[192,384]{1,0:T(8,128)}, f32[192,384]{1,0:T(8,128)}) custom-call(bf16[96,128]{1,0:T(8,128)(2,1)S(1)} %get-tuple-element.9.ig, f32[192,384]{1,0:T(8,128)S(1)} %get-tuple-element.10.nmi, f32[192,384]{1,0:T(8,128)S(1)} %get-tuple-element.11.nmo), custom_call_target="tpu_custom_call" | custom-call | tf_op jit(solution)/shard_map/put_out/pallas_call | solution.py:530
